TPU v7x, 32 devices: a whole 2x2x4 slice. The times are simulated.
32 devices in a mesh: tm: 4 (over y, x), sky: 8 (over z, core).
Axes of the slice: x: 2, y: 2, z: 4, core: 2. Of those that a mesh axis runs over, the one named last changes fastest.
Arguments:
- residual: float32 [16384, 128], P(('tm', 'sky')), may hold values from -110 to 110
- obs_weight: float32 [16384, 128], P(('tm', 'sky')), may hold values from 0.5 to 2
- source_partials: float32 [5, 16384, 128], P(None, ('tm', 'sky')), may hold values from -1 to 1
- attitude_partials: float32 [16, 16384, 128], P(None, ('tm', 'sky')), may hold values from -1.5 to 1.5
- source_index: int32 [16384, 128], P(('tm', 'sky')), may hold values from 0 to 127
- tile_pixel: int32 [16384], P(('tm', 'sky')), may hold values from 0 to 1023, as said below
- tile_knot: int32 [16384], P(('tm', 'sky')), may hold values from 0 to 2047, as said below
- pixel_slot: int32 [1024], replicated, may hold values from 0 to 1023, as said below
Outputs:
- final_residual: float32 [16384, 128], P(('tm', 'sky'))
- source_update: float32 [5, 131072], P(None, 'sky')
- attitude_update: float32 [4, 2048], P(None, 'tm')
Inputs may be any that keep to these rules, and one draw needn't show every extreme that they name: Tiles come in aligned blocks of 512; with owner = pixel_slot[tile_pixel[t]] // 128, no block holds more than 192 tiles of one owner, and every block holds exactly 192 tiles of some owner. `pixel_slot`: every slot number appears once. `tile_knot`: the tiles of aligned block q of 512 tiles have first knots in [q * 64, (q + 1) * 64).
All inputs are finite; a program needn't handle non-finite values.
Results may differ from a plain program's by a relative error of at most 0.0003.
Values sent between devices are 32-bit elements; how exact they have to be, the bound alone decides.
No kernel may reach another device: no remote copies, remote signals or barrier semaphores. Data moves between devices by JAX's collectives and lax.ppermute only.
A program may use at most 128 MiB of HBM per device.

v0:
```python
import math
import jax
import jax.numpy as jnp
from jax import lax
from jax.sharding import PartitionSpec as P

PIX_DEV = 128
SRC_PIX = 128
KNOTS_DEV = 512
SOURCE_PAIRS = tuple(((first, second) for first in range(5) for second in range(first, 5)))
KNOT_PAIRS = tuple(((first, second) for first in range(4) for second in range(first, 4)))


def passed_along(value, axis, steps):
    count = lax.axis_size(axis)
    first, last = (max(0, -steps), min(count, count - steps))
    return lax.ppermute(value, axis, [(source, source + steps) for source in range(first, last)])


def damped_solve(normal, target, order, pairs):
    entries = {}
    for number, couple in enumerate(pairs):
        entries[couple] = normal[number]
    factor = {}
    for column in range(order):
        pivot_value = entries[column, column] + 1.0
        for earlier in range(column):
            pivot_value = pivot_value - factor[column, earlier] * factor[column, earlier]
        pivot_value = jnp.sqrt(pivot_value)
        factor[column, column] = pivot_value
        for below in range(column + 1, order):
            current = entries[column, below]
            for earlier in range(column):
                current = current - factor[below, earlier] * factor[column, earlier]
            factor[below, column] = current / pivot_value
    forward = []
    for column in range(order):
        current = target[column]
        for earlier in range(column):
            current = current - factor[column, earlier] * forward[earlier]
        forward.append(current / factor[column, column])
    answer = [None] * order
    for column in reversed(range(order)):
        current = forward[column]
        for later in range(column + 1, order):
            current = current - factor[later, column] * answer[later]
        answer[column] = current / factor[column, column]
    return jnp.stack(answer)


def knot_terms(weights, partials, baseline):
    result = []
    for segment in range(4):
        portion = partials[4 * segment : 4 * segment + 4]
        sums_rows = [
            jnp.sum(weights * portion[first] * portion[second], axis=-1)
            for first, second in KNOT_PAIRS
        ]
        sums_rows = sums_rows + [
            jnp.sum(weights * portion[first] * baseline, axis=-1) for first in range(4)
        ]
        result.append(jnp.stack(sums_rows))
    return result


def correct(baseline, partials, picked):
    accumulated = partials[0] * picked[0]
    for component in range(1, partials.shape[0]):
        accumulated = accumulated + partials[component] * picked[component]
    return baseline - accumulated


def pixel_sums(products, indices, owners, capacity):

    def add_sender(sender, running):
        offset = sender * capacity
        portion = lax.dynamic_slice_in_dim(products, offset, capacity, 1)
        chosen = lax.dynamic_slice_in_dim(indices, offset, capacity, 0)
        within = ((chosen % SRC_PIX)[:, :, None] == jnp.arange(SRC_PIX, dtype=jnp.int32)).astype(
            jnp.float32
        )
        pixel_hits = (
            (chosen[:, 0] // SRC_PIX)[:, None] == jnp.arange(PIX_DEV, dtype=jnp.int32)
        ).astype(jnp.float32)
        spread = jnp.einsum("ctk,tks->cts", portion, within, precision=lax.Precision.HIGHEST)
        return running + jnp.einsum(
            "cts,tp->cps", spread, pixel_hits, precision=lax.Precision.HIGHEST
        )

    running = lax.fori_loop(0, owners, add_sender, jnp.zeros((20, PIX_DEV, SRC_PIX), jnp.float32))
    return running.reshape(20, PIX_DEV * SRC_PIX)


def pick_sources(update, indices, rows):
    pixels = update.shape[1] // SRC_PIX
    table = update.reshape(update.shape[0], pixels, SRC_PIX)
    blocks = indices.shape[0] // rows

    def fill(number, output):
        offset = number * rows
        chosen = lax.dynamic_slice_in_dim(indices, offset, rows, 0)
        pixel_hits = (
            (chosen[:, 0] // SRC_PIX)[:, None] == jnp.arange(pixels, dtype=jnp.int32)
        ).astype(jnp.float32)
        within = ((chosen % SRC_PIX)[:, :, None] == jnp.arange(SRC_PIX, dtype=jnp.int32)).astype(
            jnp.float32
        )
        row_values = jnp.einsum("tp,cps->cts", pixel_hits, table, precision=lax.Precision.HIGHEST)
        picked = jnp.einsum("cts,tks->ctk", row_values, within, precision=lax.Precision.HIGHEST)
        return lax.dynamic_update_slice_in_dim(output, picked, offset, 1)

    empty = jnp.zeros((update.shape[0], indices.shape[0], indices.shape[1]), jnp.float32)
    return lax.fori_loop(0, blocks, fill, empty)


def body(
    residual,
    obs_weight,
    source_partials,
    attitude_partials,
    source_index,
    tile_pixel,
    tile_knot,
    pixel_slot,
):
    owners = lax.axis_size("sky")
    tiles = residual.shape[0]
    capacity = 3 * tiles // owners
    pixels = pixel_slot.shape[0]
    pixel_match = (tile_pixel[:, None] == jnp.arange(pixels, dtype=jnp.int32)[None, :]).astype(
        jnp.float32
    )
    seats_float = jnp.dot(
        pixel_match, pixel_slot.astype(jnp.float32), precision=lax.Precision.HIGHEST
    )
    seats = seats_float.astype(jnp.int32)
    owner_ids = seats // PIX_DEV
    local_pixel = seats % PIX_DEV
    member = (owner_ids[:, None] == jnp.arange(owners, dtype=jnp.int32)[None, :]).astype(
        jnp.float32
    )
    tile_numbers = jnp.arange(tiles, dtype=jnp.int32)
    lower = (tile_numbers[:, None] > tile_numbers[None, :]).astype(jnp.float32)
    before = jnp.dot(lower, member, precision=lax.Precision.HIGHEST)
    position = jnp.sum(before * member, axis=1).astype(jnp.int32)
    slot_index = owner_ids * capacity + position
    place = (jnp.arange(owners * capacity, dtype=jnp.int32)[:, None] == slot_index[None, :]).astype(
        jnp.float32
    )
    local_source = (local_pixel[:, None] * SRC_PIX + source_index).astype(jnp.float32)
    sent_index = jnp.dot(place, local_source, precision=lax.Precision.HIGHEST).astype(jnp.int32)[
        None
    ]
    root_weight = jnp.sqrt(obs_weight)
    fields = jnp.concatenate(
        [(root_weight * residual)[None], root_weight[None] * source_partials], axis=0
    )
    packed = jnp.einsum("st,ctk->csk", place, fields, precision=lax.Precision.HIGHEST)
    arrived, arrived_index = (
        lax.all_to_all(packed, "sky", split_axis=1, concat_axis=1, tiled=True),
        lax.all_to_all(sent_index, "sky", split_axis=1, concat_axis=1, tiled=True),
    )
    scaled = arrived[1:]
    products = [scaled[first] * scaled[second] for first, second in SOURCE_PAIRS]
    products = jnp.stack(products + [scaled[first] * arrived[0] for first in range(5)])
    normals = pixel_sums(products, arrived_index[0], owners, capacity)
    summed = lax.psum(normals, "tm")
    source_update = damped_solve(summed[:15], summed[15:], 5, SOURCE_PAIRS)
    everything = lax.all_gather(source_update, "sky", axis=1, tiled=True)
    global_source = seats[:, None] * SRC_PIX + source_index
    picked = pick_sources(everything, global_source, math.gcd(tiles, 64))
    settled = correct(residual, source_partials, picked)
    knot_start = tile_knot - lax.axis_index("tm") * KNOTS_DEV
    knot_hits = (knot_start[:, None] == jnp.arange(KNOTS_DEV, dtype=jnp.int32)[None, :]).astype(
        jnp.float32
    )
    accumulated = jnp.zeros((14, KNOTS_DEV + 3), jnp.float32)
    for segment, tile_sums in enumerate(knot_terms(obs_weight, attitude_partials, settled)):
        placed = jnp.dot(tile_sums, knot_hits, precision=lax.Precision.HIGHEST)
        accumulated = accumulated + jnp.pad(placed, ((0, 0), (segment, 3 - segment)))
    arriving = passed_along(accumulated[:, KNOTS_DEV:], "tm", 1)
    own_rows = accumulated[:, :KNOTS_DEV] + jnp.pad(arriving, ((0, 0), (0, KNOTS_DEV - 3)))
    whole = lax.psum(own_rows, "sky")
    attitude_update = damped_solve(whole[:10], whole[10:], 4, KNOT_PAIRS)
    following = passed_along(attitude_update[:, :3], "tm", -1)
    extended = jnp.concatenate([attitude_update, following], axis=1)
    accumulated_fix = None
    for segment in range(4):
        window = extended[:, segment : segment + KNOTS_DEV]
        values = jnp.dot(window, knot_hits.T, precision=lax.Precision.HIGHEST)
        for component in range(4):
            addend = attitude_partials[4 * segment + component] * values[component][:, None]
            accumulated_fix = addend if accumulated_fix is None else accumulated_fix + addend
    final_residual = settled - accumulated_fix
    return (final_residual, source_update, attitude_update)


def solution(mesh):
    in_specs = (
        P(("tm", "sky"), None),
        P(("tm", "sky"), None),
        P(None, ("tm", "sky"), None),
        P(None, ("tm", "sky"), None),
        P(("tm", "sky"), None),
        P(("tm", "sky")),
        P(("tm", "sky")),
        P(),
    )
    out_specs = (P(("tm", "sky"), None), P(None, "sky"), P(None, "tm"))
    return jax.shard_map(body, mesh=mesh, in_specs=in_specs, out_specs=out_specs, check_vma=False)
```

profile of v0, /device:TPU:0, one launch (start us, length us, event | category | flops | bytes accessed | tf_op | source)
XLA Modules:
  0.0 626.5 jit_solution(8565217620249601764)
XLA Ops:
  8.0 1.8 fusion.32
  10.0 1.1 copy.41
  12.9 6.0 convolution_bitcast_fusion.1
  18.8 6.2 copy.44
  25.0 6.5 %all-to-all-start.1 = ((f32[6,1536,128]{2,0,1:T(8,128)}), f32[6,1536,128]{2,0,1:T(8,128)}, u32[]{:S(2)}, u32[]{:S(2)}) async-start(f32[6,1536,128]{2,0,1:T(8,128)} %copy.44), calls=%async_computation.1 | async-start | bytes 12582912 | tf_op jit(solution)/shard_map/all_to_all | solution.py:160
  31.5 2.5 fusion.31
  34.0 136.5 %all-to-all-done.1 = f32[6,1536,128]{2,0,1:T(8,128)} async-done(((f32[6,1536,128]{2,0,1:T(8,128)}), f32[6,1536,128]{2,0,1:T(8,128)}, u32[]{:S(2)}, u32[]{:S(2)}) %all-to-all-start.1) | async-done | bytes 4718624 | tf_op jit(solution)/shard_map/all_to_all | solution.py:160
  170.5 4.2 all-to-all-start
  175.0 22.1 %slice_multiply_fusion = (f32[1,1536,128]{2,0,1:T(1,128)S(1)}, f32[1,1536,128]{2,0,1:T(1,128)S(1)}, f32[1,1536,128]{2,0,1:T(1,128)}, f32[1,1536,128]{2,0,1:T(1,1...) fusion(f32[6,1536,128]{2,0,1:T(8,128)} %all-to-all-done.1), kind=kLoop, calls=%fused_computation.340 | loop fusion | flops 2359296 | bytes 14155776 | tf_op jit(solution)/shard_map/mul | solution.py:165
  197.1 20.9 %slice_multiply_fusion.1 = (f32[1,1536,128]{2,0,1:T(1,128)}, f32[1,1536,128]{2,0,1:T(1,128)}, f32[1,1536,128]{2,0,1:T(1,128)}, f32[1,1536,128]{2,0,1:T(1,128)}, ...) fusion(f32[6,1536,128]{2,0,1:T(8,128)} %all-to-all-done.1), kind=kLoop, calls=%fused_computation.341 | loop fusion | flops 1572864 | bytes 11010048 | tf_op jit(solution)/shard_map/mul | solution.py:165
  218.0 49.6 %stack.218 = f32[20,1536,128]{2,0,1:T(8,128)} concatenate(f32[1,1536,128]{2,0,1:T(1,128)} %get-tuple-element.400, f32[1,1536,128]{2,0,1:T(1,128)} %get-tuple-element.408, f32[1,1536,128]{2,0,1:T(1,128)} %get-tuple-element.407, f32[1,1536,128]{2,0,1:T(1,128)} %get-tuple-element.406, f32[1,1536,128]{2,0,1:T(1,128)} %get-tuple-element.405, f32[1,1536,128]{2,0,1:T(1,128)S(1)} %get-tuple-element.390, ...), dimensions={0} | concatenate | bytes 31457280 | tf_op jit(solution)/shard_map/stack | solution.py:165
  267.7 114.9 %while.32 = (s32[]{:T(128)}, f32[20,128,128]{2,1,0:T(8,128)S(1)}, s32[1536,128]{1,0:T(8,128)}, f32[20,1536,128]{2,0,1:T(8,128)}, s32[]{:T(128)}, /*index=5*/s32[]{:T(128)}, s32[]{:T(128)}, s32[]{:T(128)}) while((s32[]{:T(128)}, f32[20,128,128]{2,1,0:T(8,128)S(1)}, s32[1536,128]{1,0:T(8,128)}, f32[20,1536,128]{2,0,1:T(8,128)}, ...), condition=%wide.region_2.3_spmd.clone, body=%wide.region_1.2_spmd.clone.sunk | while | flops 1514048256 | bytes 9800085 | solution.py:90
  268.8 9.9 %fusion.206 = f32[20,192,128]{2,0,1:T(8,128)} fusion(f32[20,1536,128]{2,0,1:T(8,128)} %get-tuple-element.501, s32[]{:T(128)S(6)} %select_n.124, s32[192,128]{1,0:T(8,128)S(1)} %copy.140), kind=kOutput, calls=%fused_computation.26.clone.1 | convolution fusion | flops 758120448 | bytes 4423684 | tf_op jit(solution)/shard_map/while/body/eval_jaxpr/ctk,tks->cts/dot_general | solution.py:85
  278.8 3.2 fusion.207
  283.2 9.9 %fusion.206 = f32[20,192,128]{2,0,1:T(8,128)} fusion(f32[20,1536,128]{2,0,1:T(8,128)} %get-tuple-element.501, s32[]{:T(128)S(6)} %select_n.124, s32[192,128]{1,0:T(8,128)S(1)} %copy.140), kind=kOutput, calls=%fused_computation.26.clone.1 | convolution fusion | flops 758120448 | bytes 4423684 | tf_op jit(solution)/shard_map/while/body/eval_jaxpr/ctk,tks->cts/dot_general | solution.py:85
  293.1 3.2 fusion.207
  297.6 9.9 %fusion.206 = f32[20,192,128]{2,0,1:T(8,128)} fusion(f32[20,1536,128]{2,0,1:T(8,128)} %get-tuple-element.501, s32[]{:T(128)S(6)} %select_n.124, s32[192,128]{1,0:T(8,128)S(1)} %copy.140), kind=kOutput, calls=%fused_computation.26.clone.1 | convolution fusion | flops 758120448 | bytes 4423684 | tf_op jit(solution)/shard_map/while/body/eval_jaxpr/ctk,tks->cts/dot_general | solution.py:85
  307.5 3.2 fusion.207
  311.9 9.9 %fusion.206 = f32[20,192,128]{2,0,1:T(8,128)} fusion(f32[20,1536,128]{2,0,1:T(8,128)} %get-tuple-element.501, s32[]{:T(128)S(6)} %select_n.124, s32[192,128]{1,0:T(8,128)S(1)} %copy.140), kind=kOutput, calls=%fused_computation.26.clone.1 | convolution fusion | flops 758120448 | bytes 4423684 | tf_op jit(solution)/shard_map/while/body/eval_jaxpr/ctk,tks->cts/dot_general | solution.py:85
  321.9 3.2 fusion.207
  326.3 9.9 %fusion.206 = f32[20,192,128]{2,0,1:T(8,128)} fusion(f32[20,1536,128]{2,0,1:T(8,128)} %get-tuple-element.501, s32[]{:T(128)S(6)} %select_n.124, s32[192,128]{1,0:T(8,128)S(1)} %copy.140), kind=kOutput, calls=%fused_computation.26.clone.1 | convolution fusion | flops 758120448 | bytes 4423684 | tf_op jit(solution)/shard_map/while/body/eval_jaxpr/ctk,tks->cts/dot_general | solution.py:85
  336.2 3.2 fusion.207
  340.6 9.9 %fusion.206 = f32[20,192,128]{2,0,1:T(8,128)} fusion(f32[20,1536,128]{2,0,1:T(8,128)} %get-tuple-element.501, s32[]{:T(128)S(6)} %select_n.124, s32[192,128]{1,0:T(8,128)S(1)} %copy.140), kind=kOutput, calls=%fused_computation.26.clone.1 | convolution fusion | flops 758120448 | bytes 4423684 | tf_op jit(solution)/shard_map/while/body/eval_jaxpr/ctk,tks->cts/dot_general | solution.py:85
  350.6 3.2 fusion.207
  355.0 9.9 %fusion.206 = f32[20,192,128]{2,0,1:T(8,128)} fusion(f32[20,1536,128]{2,0,1:T(8,128)} %get-tuple-element.501, s32[]{:T(128)S(6)} %select_n.124, s32[192,128]{1,0:T(8,128)S(1)} %copy.140), kind=kOutput, calls=%fused_computation.26.clone.1 | convolution fusion | flops 758120448 | bytes 4423684 | tf_op jit(solution)/shard_map/while/body/eval_jaxpr/ctk,tks->cts/dot_general | solution.py:85
  365.0 3.2 fusion.207
  369.4 9.9 %fusion.206 = f32[20,192,128]{2,0,1:T(8,128)} fusion(f32[20,1536,128]{2,0,1:T(8,128)} %get-tuple-element.501, s32[]{:T(128)S(6)} %select_n.124, s32[192,128]{1,0:T(8,128)S(1)} %copy.140), kind=kOutput, calls=%fused_computation.26.clone.1 | convolution fusion | flops 758120448 | bytes 4423684 | tf_op jit(solution)/shard_map/while/body/eval_jaxpr/ctk,tks->cts/dot_general | solution.py:85
  379.3 3.2 fusion.207
  382.7 2.1 copy.116
  385.1 61.7 %all-reduce.7.cloned.1.call-done = f32[20,16384]{1,0:T(8,128)} async-done(((f32[20,16384]{1,0:T(8,128)}), f32[20,16384]{1,0:T(8,128)}) %all-reduce.7.cloned.1.call-update) | async-done | bytes 1310736 | tf_op jit(solution)/shard_map/psum | solution.py:167
  446.8 5.2 fusion.141
  452.1 3.9 fusion.142
  456.0 3.9 subtract_divide_fusion
  459.8 1.2 stack.219
  461.3 3.1 fusion.102
  464.3 3.7 fusion.99
  468.1 40.0 %all-gather.2.cloned.1.call-done = f32[5,131072]{1,0:T(8,128)} async-done(((f32[5,16384]{1,0:T(8,128)}), f32[5,131072]{1,0:T(8,128)}) %all-gather.2.cloned.1.call-update) | async-done | bytes 2621456 | tf_op jit(solution)/shard_map/all_gather | solution.py:169
  508.1 2.7 copy.128
  510.8 1.1 broadcast_in_dim.32.clone
  511.9 55.2 %while.31 = (s32[]{:T(128)}, f32[5,512,128]{2,1,0:T(8,128)}, s32[512,128]{0,1:T(8,128)S(1)}, f32[5,1024,128]{2,1,0:T(8,128)S(1)}, s32[]{:T(128)}, /*index=5*/s32[]{:T(128)}, s32[]{:T(128)}, s32[]{:T(128)}) while((s32[]{:T(128)}, f32[5,512,128]{2,1,0:T(8,128)}, s32[512,128]{0,1:T(8,128)S(1)}, f32[5,1024,128]{2,1,0:T(8,128)S(1)}, s32[]{:T(128)}, ...), condition=%wide.region_5.6_spmd, body=%wide.region_4.5_spmd.sunk | while | flops 567436224 | bytes 3605391 | solution.py:113
  512.0 1.2 convolution_bitcast_fusion.3
  513.4 4.8 fusion.202
  518.9 1.2 convolution_bitcast_fusion.3
  520.2 4.8 fusion.202
  525.8 1.2 convolution_bitcast_fusion.3
  527.1 4.8 fusion.202
  532.7 1.2 convolution_bitcast_fusion.3
  534.1 4.8 fusion.202
  539.6 1.2 convolution_bitcast_fusion.3
  541.0 4.8 fusion.202
  546.5 1.2 convolution_bitcast_fusion.3
  547.8 4.8 fusion.202
  553.4 1.2 convolution_bitcast_fusion.3
  554.8 4.8 fusion.202
  560.3 1.2 convolution_bitcast_fusion.3
  561.7 4.8 fusion.202
  567.2 3.6 multiply_reduce_fusion.12
  571.1 2.3 fusion.85
  575.8 3.4 collective-permute-start
  579.2 1.2 collective-permute-done
  580.5 25.9 %psum.15 = f32[14,512]{1,0:T(8,128)S(1)} all-reduce(f32[14,512]{1,0:T(8,128)S(1)} %slice_add_fusion.5), channel_id=1, replica_groups=mesh['tm'=4,'sky'=8] {'sky'}, use_global_device_ids=true, to_apply=%region_62.63 | all-reduce | flops 7168 | bytes 57344 | tf_op jit(solution)/shard_map/psum | solution.py:183
  607.3 1.3 collective-permute-start.1
  608.6 4.4 collective-permute-done.1
  615.0 4.6 fusion.61
  (137 shorter events, 26.1 us)
Async XLA Ops:
  7.2 5.1 copy-start.1
  25.0 6.5 %copy-start.8 = (s32[512,128]{1,0:T(8,128)S(1)}, s32[512,128]{1,0:T(8,128)}, u32[]{:S(2)}) copy-start(s32[512,128]{1,0:T(8,128)} %param.16) | copy-start | bytes 786436
  25.0 145.5 %all-to-all-start.1 = ((f32[6,1536,128]{2,0,1:T(8,128)}), f32[6,1536,128]{2,0,1:T(8,128)}, u32[]{:S(2)}, u32[]{:S(2)}) async-start(f32[6,1536,128]{2,0,1:T(8,128)} %copy.44), calls=%async_computation.1 | async-start | bytes 12582912 | tf_op jit(solution)/shard_map/all_to_all | solution.py:160
  170.5 97.1 %all-to-all-start = ((s32[1,1536,128]{2,0,1:T(1,128)}), s32[1,1536,128]{2,0,1:T(1,128)}, u32[]{:S(2)}, u32[]{:S(2)}) async-start(s32[1,1536,128]{2,0,1:T(1,128)} %bitcast.7), calls=%async_computation | async-start | bytes 1572864 | tf_op jit(solution)/shard_map/all_to_all | solution.py:161
  174.7 272.1 %all-reduce.7.cloned.1.call-start = ((), (), s32[]{:S(2)}) async-start(), calls=%async_computation.2 | async-start | bytes 3145728 | tf_op jit(solution)/shard_map/psum | solution.py:167
  384.8 123.3 %all-gather.2.cloned.1.call-start = ((), (), s32[]{:S(2)}) async-start(), calls=%async_computation.3 | async-start | bytes 4718592 | tf_op jit(solution)/shard_map/all_gather | solution.py:169
  456.0 5.2 copy-start.10
  456.0 5.3 copy-start.2
  567.1 3.7 copy-start
  567.1 3.7 copy-start.3
  567.1 3.8 copy-start.4
  567.1 3.9 copy-start.5
  567.1 3.9 copy-start.6
  567.1 4.0 copy-start.7
  575.8 4.7 collective-permute-start
  606.6 13.0 %copy-start.9 = (f32[4,512]{1,0:T(4,128)}, f32[4,512]{1,0:T(4,128)S(1)}, u32[]{:S(2)}) copy-start(f32[4,512]{1,0:T(4,128)S(1)} %pad_maximum_fusion.1) | copy-start | bytes 24580
  607.3 5.7 collective-permute-start.1
Sparse Core Ops, SparseCore 0:
  384.9 61.8 all-reduce.6
  461.2 46.8 all-gather.1
where the time goes:
time: 634 us; the launch traced here: 626 us
  waiting for transfers between devices  244 us (38%)
  matrix products  168 us (26%)
  local copies, waits for them, and re-layouts  81.4 us (13%)
  other arithmetic  76.7 us (12%)
  blocking collectives  25.9 us (4%)
  starting transfers between devices  15.8 us (2%)
  between operations  14.4 us (2%)
    all_to_all x1, waiting for transfers between devices, body(): lax.all_to_all(packed, 'sky', split_axis=1, concat_axis=1, tiled=True)  137 us
    dot_general x8, matrix products, add_sender(): jnp.einsum('ctk,tks->cts', portion, within, precision=lax.Precision.HIGHEST)  79.5 us
    psum x1, waiting for transfers between devices, body(): summed = lax.psum(normals, 'tm')  61.7 us
    another operation x1, local copies, waits for them, and re-layouts, body(): jnp.stack(products + [scaled[first] * arrived[0] for first in range(5)])  49.6 us
    mul x2, other arithmetic, body(): scaled[first] * arrived[0]  43.1 us
    all_gather x1, waiting for transfers between devices, body(): everything = lax.all_gather(source_update, 'sky', axis=1, tiled=True)  40 us
    dot_general x8, matrix products, fill(): jnp.einsum('cts,tks->ctk', row_values, within, precision=lax.Precision.HI...  38 us
    psum x1, blocking collectives, body(): whole = lax.psum(own_rows, 'sky')  25.9 us
  transfers between devices with their start and end apart: 6, of which 5 were waited for; matrix products, arithmetic and copies ran while one was open for 16% of the time, Pallas kernels for 0%

commit v1 on v0

--- a/solution.py
+++ b/solution.py
@@ -9,6 +9,12 @@
 KNOTS_DEV = 512
 SOURCE_PAIRS = tuple(((first, second) for first in range(5) for second in range(first, 5)))
 KNOT_PAIRS = tuple(((first, second) for first in range(4) for second in range(first, 4)))
+
+
+def stacked_exchange(x, axis, split, join):
+    cells = jnp.split(x, lax.axis_size(axis), axis=split)
+    received = lax.all_to_all(jnp.stack(cells), axis, 0, 0)
+    return jnp.concatenate(received, axis=join)
 
 
 def passed_along(value, axis, steps):
@@ -157,7 +163,7 @@
     )
     packed = jnp.einsum("st,ctk->csk", place, fields, precision=lax.Precision.HIGHEST)
     arrived, arrived_index = (
-        lax.all_to_all(packed, "sky", split_axis=1, concat_axis=1, tiled=True),
+        stacked_exchange(packed, "sky", 1, 1),
         lax.all_to_all(sent_index, "sky", split_axis=1, concat_axis=1, tiled=True),
     )
     scaled = arrived[1:]

time: 634 us -> 544 us (0.86); the launches traced: 626 us -> 543 us
  other arithmetic: 76.7 us -> 36 us
  waiting for transfers between devices: 244 us -> 211 us
  local copies, waits for them, and re-layouts: 81.4 us -> 69.9 us
    another operation x1, local copies, waits for them, and re-layouts: 49.6 us -> 0.94 us  [body(): jnp.stack(products + [scaled[first] * arrived[0] for first in range(5)])]
    mul x2, other arithmetic: 43.1 us -> 2.1 us  [body(): scaled[first] * arrived[0]]
    all_to_all x1, waiting for transfers between devices: 137 us -> 103 us  [stacked_exchange(): received = lax.all_to_all(jnp.stack(cells), axis, 0, 0)]
    unnamed x29 -> x43, local copies, waits for them, and re-layouts: 8.03 us -> 34.4 us
    dynamic_slice x0 -> x8, local copies, waits for them, and re-layouts: none -> 13.8 us  [add_sender(): portion = lax.dynamic_slice_in_dim(products, offset, capacity, 1)]
    another operation x0 -> x2, local copies, waits for them, and re-layouts: none -> 7.39 us  [stacked_exchange(): received = lax.all_to_all(jnp.stack(cells), axis, 0, 0)]
    dynamic_slice x16, local copies, waits for them, and re-layouts: 8 us -> 0.86 us  [add_sender(): chosen = lax.dynamic_slice_in_dim(indices, offset, capacity, 0)]
  transfers between devices with their start and end apart: 6 -> 6, of which waited for: 5 -> 5; matrix products, arithmetic and copies ran while one was open for 16% -> 6% of each run, Pallas kernels for 0% -> 0%
where the time goes in v1:
time: 544 us; the launch traced here: 543 us
  waiting for transfers between devices  211 us (39%)
  matrix products  171 us (31%)
  local copies, waits for them, and re-layouts  69.9 us (13%)
  other arithmetic  36 us (7%)
  blocking collectives  25.9 us (5%)
  starting transfers between devices  15 us (3%)
  between operations  14.4 us (3%)
    all_to_all x1, waiting for transfers between devices, stacked_exchange(): received = lax.all_to_all(jnp.stack(cells), axis, 0, 0)  103 us
    dot_general x8, matrix products, add_sender(): jnp.einsum('ctk,tks->cts', portion, within, precision=lax.Precision.HIGHEST)  84.4 us
    psum x1, waiting for transfers between devices, body(): summed = lax.psum(normals, 'tm')  62 us
    all_gather x1, waiting for transfers between devices, body(): everything = lax.all_gather(source_update, 'sky', axis=1, tiled=True)  40 us
    dot_general x8, matrix products, fill(): jnp.einsum('cts,tks->ctk', row_values, within, precision=lax.Precision.HI...  38 us
    unnamed x43, local copies, waits for them, and re-layouts  34.4 us
    psum x1, blocking collectives, body(): whole = lax.psum(own_rows, 'sky')  25.9 us
    dot_general x8, matrix products, add_sender(): jnp.einsum('cts,tp->cps', spread, pixel_hits, precision=lax.Precision.HIG...  25.8 us
  transfers between devices with their start and end apart: 6, of which 5 were waited for; matrix products, arithmetic and copies ran while one was open for 6% of the time, Pallas kernels for 0%

profile of v1, /device:TPU:0, one launch (start us, length us, event | category | flops | bytes accessed | tf_op | source)
XLA Modules:
  0.0 543.1 jit_solution(17409122843602557673)
XLA Ops:
  7.9 1.8 fusion.31
  12.1 1.7 copy.61
  14.1 4.1 convolution_bitcast_fusion.1
  19.1 1.2 fusion.53
  25.5 1.2 fusion.47
  26.7 6.2 %copy.62 = f32[8,6,192,128]{3,2,1,0:T(8,128)} copy(f32[8,6,192,128]{2,3,1,0:T(8,128)} %fusion.47) | data formatting | bytes 9437184 | tf_op jit(solution)/shard_map/stack | solution.py:16
  32.8 6.5 %all-to-all-start.1 = ((f32[8,6,192,128]{3,2,1,0:T(8,128)}), f32[8,6,192,128]{3,2,1,0:T(8,128)}, u32[]{:S(2)}, u32[]{:S(2)}) async-start(f32[8,6,192,128]{3,2,1,0:T(8,128)} %copy.62), calls=%async_computation.1 | async-start | bytes 9437184 | tf_op jit(solution)/shard_map/all_to_all | solution.py:16
  39.3 2.5 fusion.30
  41.8 102.8 %all-to-all-done.1 = f32[8,6,192,128]{3,2,1,0:T(8,128)} async-done(((f32[8,6,192,128]{3,2,1,0:T(8,128)}), f32[8,6,192,128]{3,2,1,0:T(8,128)}, u32[]{:S(2)}, u32[]{:S(2)}) %all-to-all-start.1) | async-done | bytes 4718624 | tf_op jit(solution)/shard_map/all_to_all | solution.py:16
  144.7 3.5 all-to-all-start
  148.4 2.6 copy.154
  151.1 1.3 slice_multiply_fusion
  172.2 126.6 %while.32 = (s32[]{:T(128)}, f32[20,128,128]{2,1,0:T(8,128)S(1)}, s32[1536,128]{1,0:T(8,128)S(1)}, f32[20,1536,128]{2,1,0:T(8,128)}, s32[]{:T(128)}, /*index=5*/s32[]{:T(128)}, s32[]{:T(128)}, s32[]{:T(128)}) while((s32[]{:T(128)}, f32[20,128,128]{2,1,0:T(8,128)S(1)}, s32[1536,128]{1,0:T(8,128)S(1)}, f32[20,1536,128]{2,1,0:T(8,128)}, ...), condition=%wide.region_2.3_spmd.clone, body=%wide.region_1.2_spmd.clone.sunk | while | flops 1514048256 | bytes 13339029 | solution.py:96
  172.5 1.7 constant_dynamic-slice_fusion.5
  174.2 10.5 %fusion.213 = f32[20,192,128]{2,0,1:T(8,128)} fusion(f32[20,192,128]{2,1,0:T(8,128)S(1)} %constant_dynamic-slice_fusion.5, s32[192,128]{1,0:T(8,128)S(1)} %copy.169), kind=kOutput, calls=%fused_computation.26.clone.1 | convolution fusion | flops 758120448 | bytes 4030464 | tf_op jit(solution)/shard_map/while/body/eval_jaxpr/ctk,tks->cts/dot_general | solution.py:91
  184.8 3.2 fusion.214
  188.3 1.7 constant_dynamic-slice_fusion.5
  190.0 10.5 %fusion.213 = f32[20,192,128]{2,0,1:T(8,128)} fusion(f32[20,192,128]{2,1,0:T(8,128)S(1)} %constant_dynamic-slice_fusion.5, s32[192,128]{1,0:T(8,128)S(1)} %copy.169), kind=kOutput, calls=%fused_computation.26.clone.1 | convolution fusion | flops 758120448 | bytes 4030464 | tf_op jit(solution)/shard_map/while/body/eval_jaxpr/ctk,tks->cts/dot_general | solution.py:91
  200.6 3.2 fusion.214
  204.1 1.7 constant_dynamic-slice_fusion.5
  205.9 10.5 %fusion.213 = f32[20,192,128]{2,0,1:T(8,128)} fusion(f32[20,192,128]{2,1,0:T(8,128)S(1)} %constant_dynamic-slice_fusion.5, s32[192,128]{1,0:T(8,128)S(1)} %copy.169), kind=kOutput, calls=%fused_computation.26.clone.1 | convolution fusion | flops 758120448 | bytes 4030464 | tf_op jit(solution)/shard_map/while/body/eval_jaxpr/ctk,tks->cts/dot_general | solution.py:91
  216.4 3.2 fusion.214
  220.0 1.7 constant_dynamic-slice_fusion.5
  221.7 10.5 %fusion.213 = f32[20,192,128]{2,0,1:T(8,128)} fusion(f32[20,192,128]{2,1,0:T(8,128)S(1)} %constant_dynamic-slice_fusion.5, s32[192,128]{1,0:T(8,128)S(1)} %copy.169), kind=kOutput, calls=%fused_computation.26.clone.1 | convolution fusion | flops 758120448 | bytes 4030464 | tf_op jit(solution)/shard_map/while/body/eval_jaxpr/ctk,tks->cts/dot_general | solution.py:91
  232.3 3.2 fusion.214
  235.8 1.7 constant_dynamic-slice_fusion.5
  237.5 10.5 %fusion.213 = f32[20,192,128]{2,0,1:T(8,128)} fusion(f32[20,192,128]{2,1,0:T(8,128)S(1)} %constant_dynamic-slice_fusion.5, s32[192,128]{1,0:T(8,128)S(1)} %copy.169), kind=kOutput, calls=%fused_computation.26.clone.1 | convolution fusion | flops 758120448 | bytes 4030464 | tf_op jit(solution)/shard_map/while/body/eval_jaxpr/ctk,tks->cts/dot_general | solution.py:91
  248.1 3.2 fusion.214
  251.6 1.7 constant_dynamic-slice_fusion.5
  253.4 10.5 %fusion.213 = f32[20,192,128]{2,0,1:T(8,128)} fusion(f32[20,192,128]{2,1,0:T(8,128)S(1)} %constant_dynamic-slice_fusion.5, s32[192,128]{1,0:T(8,128)S(1)} %copy.169), kind=kOutput, calls=%fused_computation.26.clone.1 | convolution fusion | flops 758120448 | bytes 4030464 | tf_op jit(solution)/shard_map/while/body/eval_jaxpr/ctk,tks->cts/dot_general | solution.py:91
  263.9 3.2 fusion.214
  267.5 1.7 constant_dynamic-slice_fusion.5
  269.2 10.5 %fusion.213 = f32[20,192,128]{2,0,1:T(8,128)} fusion(f32[20,192,128]{2,1,0:T(8,128)S(1)} %constant_dynamic-slice_fusion.5, s32[192,128]{1,0:T(8,128)S(1)} %copy.169), kind=kOutput, calls=%fused_computation.26.clone.1 | convolution fusion | flops 758120448 | bytes 4030464 | tf_op jit(solution)/shard_map/while/body/eval_jaxpr/ctk,tks->cts/dot_general | solution.py:91
  279.8 3.2 fusion.214
  283.3 1.7 constant_dynamic-slice_fusion.5
  285.0 10.5 %fusion.213 = f32[20,192,128]{2,0,1:T(8,128)} fusion(f32[20,192,128]{2,1,0:T(8,128)S(1)} %constant_dynamic-slice_fusion.5, s32[192,128]{1,0:T(8,128)S(1)} %copy.169), kind=kOutput, calls=%fused_computation.26.clone.1 | convolution fusion | flops 758120448 | bytes 4030464 | tf_op jit(solution)/shard_map/while/body/eval_jaxpr/ctk,tks->cts/dot_general | solution.py:91
  295.6 3.2 fusion.214
  299.0 2.1 copy.137
  301.1 62.0 %all-reduce.7.cloned.1.call-done = f32[20,16384]{1,0:T(8,128)} async-done(((f32[20,16384]{1,0:T(8,128)}), f32[20,16384]{1,0:T(8,128)}) %all-reduce.7.cloned.1.call-update) | async-done | bytes 1310736 | tf_op jit(solution)/shard_map/psum | solution.py:173
  363.1 5.2 fusion.148
  368.4 3.9 fusion.149
  372.3 3.9 subtract_divide_fusion
  376.1 1.4 stack.255
  377.8 3.1 fusion.109
  380.9 3.7 fusion.106
  384.6 40.0 %all-gather.2.cloned.1.call-done = f32[5,131072]{1,0:T(8,128)} async-done(((f32[5,16384]{1,0:T(8,128)}), f32[5,131072]{1,0:T(8,128)}) %all-gather.2.cloned.1.call-update) | async-done | bytes 2621456 | tf_op jit(solution)/shard_map/all_gather | solution.py:175
  424.6 2.7 copy.155
  428.4 55.2 %while.31 = (s32[]{:T(128)}, f32[5,512,128]{2,1,0:T(8,128)}, s32[512,128]{0,1:T(8,128)S(1)}, f32[5,1024,128]{2,1,0:T(8,128)S(1)}, s32[]{:T(128)}, /*index=5*/s32[]{:T(128)}, s32[]{:T(128)}, s32[]{:T(128)}) while((s32[]{:T(128)}, f32[5,512,128]{2,1,0:T(8,128)}, s32[512,128]{0,1:T(8,128)S(1)}, f32[5,1024,128]{2,1,0:T(8,128)S(1)}, s32[]{:T(128)}, ...), condition=%wide.region_5.6_spmd, body=%wide.region_4.5_spmd.sunk | while | flops 567436224 | bytes 3605391 | solution.py:119
  429.9 4.8 fusion.209
  436.8 4.8 fusion.209
  443.7 4.8 fusion.209
  450.6 4.8 fusion.209
  457.5 4.8 fusion.209
  464.4 4.8 fusion.209
  471.3 4.8 fusion.209
  478.2 4.8 fusion.209
  483.6 3.6 multiply_reduce_fusion.12
  487.3 2.7 fusion.92
  492.3 3.4 collective-permute-start
  495.8 1.2 collective-permute-done
  497.1 25.9 %psum.15 = f32[14,512]{1,0:T(8,128)S(1)} all-reduce(f32[14,512]{1,0:T(8,128)S(1)} %slice_add_fusion.5), channel_id=1, replica_groups=mesh['tm'=4,'sky'=8] {'sky'}, use_global_device_ids=true, to_apply=%region_62.63 | all-reduce | flops 7168 | bytes 57344 | tf_op jit(solution)/shard_map/psum | solution.py:189
  523.9 1.3 collective-permute-start.1
  525.2 4.4 collective-permute-done.1
  531.6 4.6 fusion.68
  (161 shorter events, 55.4 us)
Async XLA Ops:
  32.8 6.5 %copy-start.2 = (s32[512,128]{1,0:T(8,128)S(1)}, s32[512,128]{1,0:T(8,128)}, u32[]{:S(2)}) copy-start(s32[512,128]{1,0:T(8,128)} %param.16) | copy-start | bytes 786436
  32.8 111.8 %all-to-all-start.1 = ((f32[8,6,192,128]{3,2,1,0:T(8,128)}), f32[8,6,192,128]{3,2,1,0:T(8,128)}, u32[]{:S(2)}, u32[]{:S(2)}) async-start(f32[8,6,192,128]{3,2,1,0:T(8,128)} %copy.62), calls=%async_computation.1 | async-start | bytes 9437184 | tf_op jit(solution)/shard_map/all_to_all | solution.py:16
  144.7 27.6 %all-to-all-start = ((s32[1,1536,128]{2,0,1:T(1,128)}), s32[1,1536,128]{2,0,1:T(1,128)S(1)}, u32[]{:S(2)}, u32[]{:S(2)}) async-start(s32[1,1536,128]{2,0,1:T(1,128)} %bitcast.7), calls=%async_computation | async-start | bytes 1572864 | tf_op jit(solution)/shard_map/all_to_all | solution.py:167
  148.2 214.9 %all-reduce.7.cloned.1.call-start = ((), (), s32[]{:S(2)}) async-start(), calls=%async_computation.2 | async-start | bytes 3145728 | tf_op jit(solution)/shard_map/psum | solution.py:173
  298.8 78.9 %copy-start.4 = (s32[512]{0:T(512)S(1)}, s32[512]{0:T(512)}, u32[]{:S(2)}) copy-start(s32[512]{0:T(512)} %param.18) | copy-start | bytes 6148
  299.0 78.8 %copy-start.1 = (f32[512,128]{1,0:T(8,128)S(1)}, f32[512,128]{1,0:T(8,128)}, u32[]{:S(2)}) copy-start(f32[512,128]{1,0:T(8,128)} %param.13) | copy-start | bytes 786436
  301.1 123.5 %all-gather.2.cloned.1.call-start = ((), (), s32[]{:S(2)}) async-start(), calls=%async_computation.3 | async-start | bytes 4718592 | tf_op jit(solution)/shard_map/all_gather | solution.py:175
  483.6 3.7 copy-start
  492.3 4.7 collective-permute-start
  523.2 13.0 %copy-start.3 = (f32[4,512]{1,0:T(4,128)}, f32[4,512]{1,0:T(4,128)S(1)}, u32[]{:S(2)}) copy-start(f32[4,512]{1,0:T(4,128)S(1)} %pad_maximum_fusion.1) | copy-start | bytes 24580
  523.9 5.7 %collective-permute-start.1 = (f32[4,3]{1,0:T(4,128)S(1)}, f32[4,3]{1,0:T(4,128)S(1)}, u32[]{:S(2)}, u32[]{:S(2)}) collective-permute-start(f32[4,3]{1,0:T(4,128)S(1)} %slice.620), channel_id=1, source_target_pairs={{8,0},{16,8},{24,16},{9,1},{17,9},{25,17},{10,2},{18,10},{26,18},{... | collective-permute-start | bytes 152 | tf_op jit(solution)/shard_map/ppermute | solution.py:23
Sparse Core Ops, SparseCore 0:
  301.2 61.8 all-reduce.6
  377.7 46.8 all-gather.1
